TPU v7x, 32 devices: a whole 2x2x4 slice. The times are simulated.
32 devices in a mesh: stage: 4 (over z), data: 8 (over y, x, core).
Axes of the slice: x: 2, y: 2, z: 4, core: 2. Of those that a mesh axis runs over, the one named last changes fastest.
Arguments:
- tokens_in: bfloat16 [32, 64, 1536], P('data')
- targets: bfloat16 [32, 64, 1536], P('data')
- w_up: bfloat16 [4, 1536, 8960], P('stage')
- w_down: bfloat16 [4, 8960, 1536], P('stage')
- clip_norm: float32 [], replicated
Outputs:
- output 1: float32 [], replicated
- output 2: float32 [4, 1536, 8960], P('stage', 'data')
- output 3: float32 [4, 8960, 1536], P('stage', None, 'data')
All inputs are finite; a program needn't handle non-finite values.
Results may differ from a plain program's by a relative error of at most 0.00741393.
Values are sent between devices in bfloat16 or wider.
A program may use at most 1 GiB of HBM per device.

v0:
```python
import jax
import jax.numpy as jnp
from jax import lax
from jax.sharding import PartitionSpec as P


def layer_fwd(hidden, w_up_l, w_down_l):
    up_val = jnp.einsum("td,df->tf", hidden, w_up_l, preferred_element_type=jnp.float32)
    gelu_out = jax.nn.gelu(up_val).astype(jnp.bfloat16)
    branch = jnp.einsum("tf,fd->td", gelu_out, w_down_l, preferred_element_type=jnp.float32)
    return (hidden.astype(jnp.float32) + branch).astype(jnp.bfloat16)


def layer_bwd(hidden, g_out, w_up_l, w_down_l):
    up_val = jnp.einsum("td,df->tf", hidden, w_up_l, preferred_element_type=jnp.float32)
    gelu_val, gelu_vjp = jax.vjp(jax.nn.gelu, up_val)
    gelu_out = gelu_val.astype(jnp.bfloat16)
    grad_down_l = jnp.einsum("tf,td->fd", gelu_out, g_out, preferred_element_type=jnp.float32)
    grad_act = jnp.einsum("td,fd->tf", g_out, w_down_l, preferred_element_type=jnp.float32)
    grad_pre = gelu_vjp(grad_act)[0].astype(jnp.bfloat16)
    grad_up_l = jnp.einsum("td,tf->df", hidden, grad_pre, preferred_element_type=jnp.float32)
    back_prop = jnp.einsum("tf,df->td", grad_pre, w_up_l, preferred_element_type=jnp.float32)
    g_in = (g_out.astype(jnp.float32) + back_prop).astype(jnp.bfloat16)
    return g_in, grad_up_l, grad_down_l


def solution(mesh):
    n_stages = mesh.shape["stage"]
    n_data = mesh.shape["data"]
    fwd_perm = [(src_idx, src_idx + 1) for src_idx in range(n_stages - 1)]
    bwd_perm = [(src_idx + 1, src_idx) for src_idx in range(n_stages - 1)]

    def device_step(tokens_in, targets, w_up, w_down, clip_norm):
        n_micro, n_tokens, model_dim = tokens_in.shape
        stage_layers = w_up.shape[0]
        ffn_dim = w_up.shape[2]
        total_tokens = n_micro * n_tokens * n_data
        stage_idx = lax.axis_index("stage")
        is_first = stage_idx == 0
        is_last = stage_idx == n_stages - 1
        n_ticks = n_micro + 2 * n_stages - 2

        def run_forward(hidden):
            saved_in = []
            for layer_idx in range(stage_layers):
                saved_in.append(hidden)
                hidden = layer_fwd(hidden, w_up[layer_idx], w_down[layer_idx])
            return hidden, jnp.stack(saved_in)

        def skip_forward(hidden):
            return hidden, jnp.zeros((stage_layers, n_tokens, model_dim), hidden.dtype)

        def tick_body(tick_idx, loop_state):
            recv_fwd, recv_bwd, act_stash, acc_up, acc_down, loss_sum = loop_state
            fwd_mb = tick_idx - stage_idx
            fwd_on = (fwd_mb >= 0) & (fwd_mb < n_micro)
            fwd_safe = jnp.clip(fwd_mb, 0, n_micro - 1)
            x_mb = lax.dynamic_index_in_dim(tokens_in, fwd_safe, axis=0, keepdims=False)
            h_start = jnp.where(is_first, x_mb, recv_fwd)
            h_end, saved_in = lax.cond(fwd_on, run_forward, skip_forward, h_start)
            stash_slot = jnp.where(fwd_on, fwd_mb, n_micro)
            act_stash = lax.dynamic_update_index_in_dim(act_stash, saved_in, stash_slot, 0)
            y_mb = lax.dynamic_index_in_dim(targets, fwd_safe, axis=0, keepdims=False)
            resid_err = h_end.astype(jnp.float32) - y_mb.astype(jnp.float32)
            loss_sum = loss_sum + jnp.where(is_last & fwd_on, jnp.sum(resid_err * resid_err), 0.0)
            g_top = (resid_err / total_tokens).astype(jnp.bfloat16)

            bwd_mb = tick_idx - (2 * n_stages - 2 - stage_idx)
            bwd_on = (bwd_mb >= 0) & (bwd_mb < n_micro)
            bwd_safe = jnp.clip(bwd_mb, 0, n_micro - 1)
            saved_bwd = lax.dynamic_index_in_dim(act_stash, bwd_safe, axis=0, keepdims=False)
            g_start = jnp.where(is_last, g_top, recv_bwd)

            def run_backward(operands):
                g_cur, ups_in, downs_in = operands
                ups_out = list(ups_in)
                downs_out = list(downs_in)
                for layer_idx in reversed(range(stage_layers)):
                    g_cur, grad_u, grad_d = layer_bwd(saved_bwd[layer_idx], g_cur, w_up[layer_idx], w_down[layer_idx])
                    ups_out[layer_idx] = ups_out[layer_idx] + grad_u
                    downs_out[layer_idx] = downs_out[layer_idx] + grad_d
                return g_cur, tuple(ups_out), tuple(downs_out)

            def skip_backward(operands):
                return operands

            g_send, acc_up, acc_down = lax.cond(bwd_on, run_backward, skip_backward, (g_start, acc_up, acc_down))
            recv_fwd = lax.ppermute(h_end, "stage", fwd_perm)
            recv_bwd = lax.ppermute(g_send, "stage", bwd_perm)
            return recv_fwd, recv_bwd, act_stash, acc_up, acc_down, loss_sum

        zero_act = jnp.zeros((n_tokens, model_dim), jnp.bfloat16)
        init_state = (
            zero_act,
            zero_act,
            jnp.zeros((n_micro + 1, stage_layers, n_tokens, model_dim), jnp.bfloat16),
            tuple(jnp.zeros((model_dim, ffn_dim), jnp.float32) for layer_idx in range(stage_layers)),
            tuple(jnp.zeros((ffn_dim, model_dim), jnp.float32) for layer_idx in range(stage_layers)),
            jnp.zeros((), jnp.float32),
        )
        final_state = lax.fori_loop(0, n_ticks, tick_body, init_state)
        grad_up = lax.psum_scatter(jnp.stack(final_state[3]), "data", scatter_dimension=1, tiled=True)
        grad_down = lax.psum_scatter(jnp.stack(final_state[4]), "data", scatter_dimension=2, tiled=True)
        sq_local = jnp.sum(grad_up * grad_up) + jnp.sum(grad_down * grad_down)
        sq_total = lax.psum(sq_local, ("stage", "data"))
        clip_scale = jnp.minimum(1.0, clip_norm / jnp.sqrt(sq_total))
        loss_total = lax.psum(final_state[5], ("stage", "data")) / (2 * total_tokens)
        return loss_total, grad_up * clip_scale, grad_down * clip_scale

    return jax.shard_map(
        device_step,
        mesh=mesh,
        in_specs=(P("data"), P("data"), P("stage"), P("stage"), P()),
        out_specs=(P(), P("stage", "data", None), P("stage", None, "data")),
        check_vma=False,
    )
```

profile of v0, /device:TPU:0, one launch (start us, length us, event | category | flops | bytes accessed | tf_op | source)
XLA Modules:
  0.0 1859.2 jit_solution(16331461875684699286)
XLA Ops:
  43.8 1081.1 %while.24 = (s32[]{:T(128)}, bf16[64,1536]{1,0:T(8,128)(2,1)S(1)}, bf16[64,1536]{1,0:T(8,128)(2,1)S(1)}, bf16[5,1,64,1536]{3,2,1,0:T(8,128)(2,1)}, f32[1536,8960...) while((s32[]{:T(128)}, bf16[64,1536]{1,0:T(8,128)(2,1)S(1)}, ...), condition=%wide.region_6.7_spmd, body=%wide.region_0.6_spmd.sunk | while | flops 12382339072 | bytes 375423616 | solution.py:101
  44.8 20.5 %conditional.4 = (bf16[64,1536]{1,0:T(8,128)(2,1)S(1)}, bf16[1,1,64,1536]{3,2,1,0:T(8,128)(2,1)S(1)}) conditional(s32[]{:T(128)} %convert_element_type.97, bf16[64,1536]{1,0:T(8,128)(2,1)S(1)} %bitcast_select_fusion.2, (bf16[64,1536]{1,0:T(8,128)(2,1)S(1)}, bf16[1,1536,8960]{2,1,0:T(8,128)(2,1)}, bf16[1,8960,1536]{2,1,0:T(8,128)(2,1)}) %tuple.63), branch_computations={%region_1.1_spmd, %region_2.2_spmd} | conditional | flops 3528671232 | bytes 55836688 | solution.py:60
  79.1 20.5 %conditional.4 = (bf16[64,1536]{1,0:T(8,128)(2,1)S(1)}, bf16[1,1,64,1536]{3,2,1,0:T(8,128)(2,1)S(1)}) conditional(s32[]{:T(128)} %convert_element_type.97, bf16[64,1536]{1,0:T(8,128)(2,1)S(1)} %bitcast_select_fusion.2, (bf16[64,1536]{1,0:T(8,128)(2,1)S(1)}, bf16[1,1536,8960]{2,1,0:T(8,128)(2,1)}, bf16[1,8960,1536]{2,1,0:T(8,128)(2,1)}) %tuple.63), branch_computations={%region_1.1_spmd, %region_2.2_spmd} | conditional | flops 3528671232 | bytes 55836688 | solution.py:60
  113.1 20.5 %conditional.4 = (bf16[64,1536]{1,0:T(8,128)(2,1)S(1)}, bf16[1,1,64,1536]{3,2,1,0:T(8,128)(2,1)S(1)}) conditional(s32[]{:T(128)} %convert_element_type.97, bf16[64,1536]{1,0:T(8,128)(2,1)S(1)} %bitcast_select_fusion.2, (bf16[64,1536]{1,0:T(8,128)(2,1)S(1)}, bf16[1,1536,8960]{2,1,0:T(8,128)(2,1)}, bf16[1,8960,1536]{2,1,0:T(8,128)(2,1)}) %tuple.63), branch_computations={%region_1.1_spmd, %region_2.2_spmd} | conditional | flops 3528671232 | bytes 55836688 | solution.py:60
  183.8 25.5 %collective-permute-start = (bf16[64,1536]{1,0:T(8,128)(2,1)}, bf16[64,1536]{1,0:T(8,128)(2,1)S(1)}, u32[]{:S(2)}, u32[]{:S(2)}) collective-permute-start(bf16[64,1536]{1,0:T(8,128)(2,1)} %copy-done.1), channel_id=1, source_target_pairs={{0,8},{8,16},{16,24},{1,9},{9,17},{17,25},{2,10},{10,18},{18,26},{... | collective-permute-start | bytes 589832 | tf_op jit(solution)/shard_map/while/body/eval_jaxpr/ppermute | solution.py:88
  217.2 350.3 %collective-permute-start = (bf16[64,1536]{1,0:T(8,128)(2,1)}, bf16[64,1536]{1,0:T(8,128)(2,1)S(1)}, u32[]{:S(2)}, u32[]{:S(2)}) collective-permute-start(bf16[64,1536]{1,0:T(8,128)(2,1)} %copy-done.1), channel_id=1, source_target_pairs={{0,8},{8,16},{16,24},{1,9},{9,17},{17,25},{2,10},{10,18},{18,26},{... | collective-permute-start | bytes 589832 | tf_op jit(solution)/shard_map/while/body/eval_jaxpr/ppermute | solution.py:88
  573.5 116.4 %conditional.5 = (bf16[64,1536]{1,0:T(8,128)(2,1)}, f32[1536,8960]{1,0:T(8,128)}, f32[8960,1536]{1,0:T(8,128)}) conditional(s32[]{:T(128)} %convert_element_type.98, (bf16[64,1536]{1,0:T(8,128)(2,1)S(1)}, f32[1536,8960]{1,0:T(8,128)}, f32[8960,1536]{1,0:T(8,128)}) %tuple.64, (bf16[64,1536]{1,0:T(8,128)(2,1)S(1)}, bf16[1,8960,1536]{2,1,0:T(8,128)(2,1)}, ...), branch_computations={%region_3.3_spmd, %region_4.4_spmd} | conditional | flops 8852488192 | bytes 315064416 | solution.py:87
  613.4 38.3 %convolution_add_fusion = f32[1536,8960]{1,0:T(8,128)} fusion(f32[1536,8960]{1,0:T(8,128)} %get-tuple-element.340, bf16[64,8960]{1,0:T(8,128)(2,1)S(1)} %fusion.47, bf16[5,1,64,1536]{3,2,1,0:T(8,128)(2,1)} %get-tuple-element.337, s32[]{:T(128)S(6)} %min.19), kind=kOutput, calls=%fused_computation.20 | convolution fusion | flops 1775370240 | bytes 111443968 | tf_op jit(solution)/shard_map/while/body/eval_jaxpr/cond/branch_1_fun/td,tf->df/dot_general | solution.py:21
  651.7 38.3 %convolution_add_fusion.1 = f32[8960,1536]{1,0:T(8,128)} fusion(f32[8960,1536]{1,0:T(8,128)} %get-tuple-element.341, bf16[64,1536]{1,0:T(8,128)(2,1)} %copy-done, f32[64,8960]{1,0:T(8,128)S(1)} %fusion.31), kind=kOutput, calls=%fused_computation.21 | convolution fusion | flops 1780531200 | bytes 112590848 | tf_op jit(solution)/shard_map/while/body/eval_jaxpr/cond/branch_1_fun/tf,td->fd/dot_general | solution.py:18
  691.2 25.5 %collective-permute-start = (bf16[64,1536]{1,0:T(8,128)(2,1)}, bf16[64,1536]{1,0:T(8,128)(2,1)S(1)}, u32[]{:S(2)}, u32[]{:S(2)}) collective-permute-start(bf16[64,1536]{1,0:T(8,128)(2,1)} %copy-done.1), channel_id=1, source_target_pairs={{0,8},{8,16},{16,24},{1,9},{9,17},{17,25},{2,10},{10,18},{18,26},{... | collective-permute-start | bytes 589832 | tf_op jit(solution)/shard_map/while/body/eval_jaxpr/ppermute | solution.py:88
  722.7 116.4 %conditional.5 = (bf16[64,1536]{1,0:T(8,128)(2,1)}, f32[1536,8960]{1,0:T(8,128)}, f32[8960,1536]{1,0:T(8,128)}) conditional(s32[]{:T(128)} %convert_element_type.98, (bf16[64,1536]{1,0:T(8,128)(2,1)S(1)}, f32[1536,8960]{1,0:T(8,128)}, f32[8960,1536]{1,0:T(8,128)}) %tuple.64, (bf16[64,1536]{1,0:T(8,128)(2,1)S(1)}, bf16[1,8960,1536]{2,1,0:T(8,128)(2,1)}, ...), branch_computations={%region_3.3_spmd, %region_4.4_spmd} | conditional | flops 8852488192 | bytes 315064416 | solution.py:87
  762.6 38.3 %convolution_add_fusion = f32[1536,8960]{1,0:T(8,128)} fusion(f32[1536,8960]{1,0:T(8,128)} %get-tuple-element.340, bf16[64,8960]{1,0:T(8,128)(2,1)S(1)} %fusion.47, bf16[5,1,64,1536]{3,2,1,0:T(8,128)(2,1)} %get-tuple-element.337, s32[]{:T(128)S(6)} %min.19), kind=kOutput, calls=%fused_computation.20 | convolution fusion | flops 1775370240 | bytes 111443968 | tf_op jit(solution)/shard_map/while/body/eval_jaxpr/cond/branch_1_fun/td,tf->df/dot_general | solution.py:21
  800.8 38.3 %convolution_add_fusion.1 = f32[8960,1536]{1,0:T(8,128)} fusion(f32[8960,1536]{1,0:T(8,128)} %get-tuple-element.341, bf16[64,1536]{1,0:T(8,128)(2,1)} %copy-done, f32[64,8960]{1,0:T(8,128)S(1)} %fusion.31), kind=kOutput, calls=%fused_computation.21 | convolution fusion | flops 1780531200 | bytes 112590848 | tf_op jit(solution)/shard_map/while/body/eval_jaxpr/cond/branch_1_fun/tf,td->fd/dot_general | solution.py:18
  851.4 116.4 %conditional.5 = (bf16[64,1536]{1,0:T(8,128)(2,1)}, f32[1536,8960]{1,0:T(8,128)}, f32[8960,1536]{1,0:T(8,128)}) conditional(s32[]{:T(128)} %convert_element_type.98, (bf16[64,1536]{1,0:T(8,128)(2,1)S(1)}, f32[1536,8960]{1,0:T(8,128)}, f32[8960,1536]{1,0:T(8,128)}) %tuple.64, (bf16[64,1536]{1,0:T(8,128)(2,1)S(1)}, bf16[1,8960,1536]{2,1,0:T(8,128)(2,1)}, ...), branch_computations={%region_3.3_spmd, %region_4.4_spmd} | conditional | flops 8852488192 | bytes 315064416 | solution.py:87
  891.3 38.3 %convolution_add_fusion = f32[1536,8960]{1,0:T(8,128)} fusion(f32[1536,8960]{1,0:T(8,128)} %get-tuple-element.340, bf16[64,8960]{1,0:T(8,128)(2,1)S(1)} %fusion.47, bf16[5,1,64,1536]{3,2,1,0:T(8,128)(2,1)} %get-tuple-element.337, s32[]{:T(128)S(6)} %min.19), kind=kOutput, calls=%fused_computation.20 | convolution fusion | flops 1775370240 | bytes 111443968 | tf_op jit(solution)/shard_map/while/body/eval_jaxpr/cond/branch_1_fun/td,tf->df/dot_general | solution.py:21
  929.6 38.3 %convolution_add_fusion.1 = f32[8960,1536]{1,0:T(8,128)} fusion(f32[8960,1536]{1,0:T(8,128)} %get-tuple-element.341, bf16[64,1536]{1,0:T(8,128)(2,1)} %copy-done, f32[64,8960]{1,0:T(8,128)S(1)} %fusion.31), kind=kOutput, calls=%fused_computation.21 | convolution fusion | flops 1780531200 | bytes 112590848 | tf_op jit(solution)/shard_map/while/body/eval_jaxpr/cond/branch_1_fun/tf,td->fd/dot_general | solution.py:18
  969.1 24.4 %collective-permute-start = (bf16[64,1536]{1,0:T(8,128)(2,1)}, bf16[64,1536]{1,0:T(8,128)(2,1)S(1)}, u32[]{:S(2)}, u32[]{:S(2)}) collective-permute-start(bf16[64,1536]{1,0:T(8,128)(2,1)} %copy-done.1), channel_id=1, source_target_pairs={{0,8},{8,16},{16,24},{1,9},{9,17},{17,25},{2,10},{10,18},{18,26},{... | collective-permute-start | bytes 589832 | tf_op jit(solution)/shard_map/while/body/eval_jaxpr/ppermute | solution.py:88
  999.4 116.4 %conditional.5 = (bf16[64,1536]{1,0:T(8,128)(2,1)}, f32[1536,8960]{1,0:T(8,128)}, f32[8960,1536]{1,0:T(8,128)}) conditional(s32[]{:T(128)} %convert_element_type.98, (bf16[64,1536]{1,0:T(8,128)(2,1)S(1)}, f32[1536,8960]{1,0:T(8,128)}, f32[8960,1536]{1,0:T(8,128)}) %tuple.64, (bf16[64,1536]{1,0:T(8,128)(2,1)S(1)}, bf16[1,8960,1536]{2,1,0:T(8,128)(2,1)}, ...), branch_computations={%region_3.3_spmd, %region_4.4_spmd} | conditional | flops 8852488192 | bytes 315064416 | solution.py:87
  1039.3 38.3 %convolution_add_fusion = f32[1536,8960]{1,0:T(8,128)} fusion(f32[1536,8960]{1,0:T(8,128)} %get-tuple-element.340, bf16[64,8960]{1,0:T(8,128)(2,1)S(1)} %fusion.47, bf16[5,1,64,1536]{3,2,1,0:T(8,128)(2,1)} %get-tuple-element.337, s32[]{:T(128)S(6)} %min.19), kind=kOutput, calls=%fused_computation.20 | convolution fusion | flops 1775370240 | bytes 111443968 | tf_op jit(solution)/shard_map/while/body/eval_jaxpr/cond/branch_1_fun/td,tf->df/dot_general | solution.py:21
  1077.6 38.3 %convolution_add_fusion.1 = f32[8960,1536]{1,0:T(8,128)} fusion(f32[8960,1536]{1,0:T(8,128)} %get-tuple-element.341, bf16[64,1536]{1,0:T(8,128)(2,1)} %copy-done, f32[64,8960]{1,0:T(8,128)S(1)} %fusion.31), kind=kOutput, calls=%fused_computation.21 | convolution fusion | flops 1780531200 | bytes 112590848 | tf_op jit(solution)/shard_map/while/body/eval_jaxpr/cond/branch_1_fun/tf,td->fd/dot_general | solution.py:18
  1124.9 54.5 %copy.8 = f32[8960,1536]{0,1:T(8,128)} copy(f32[8960,1536]{1,0:T(8,128)} %get-tuple-element.371) | data formatting | bytes 110100480 | tf_op jit(solution)/shard_map/while | solution.py:101
  1180.8 304.1 %reduce-scatter.5.cloned.1.call-done = f32[1,8960,192]{1,2,0:T(8,128)} async-done(((f32[1,8960,1536]{1,2,0:T(8,128)}), f32[1,8960,192]{1,2,0:T(8,128)}) %reduce-scatter.5.cloned.1.call-update) | async-done | bytes 6881296 | tf_op jit(solution)/shard_map/reduce_scatter | solution.py:103
  1490.2 302.9 %reduce-scatter.3.cloned.1.call-done = f32[1,192,8960]{2,1,0:T(8,128)} async-done(((f32[1,1536,8960]{2,1,0:T(8,128)}), f32[1,192,8960]{2,1,0:T(8,128)}) %reduce-scatter.3.cloned.1.call-update) | async-done | bytes 6881296 | tf_op jit(solution)/shard_map/reduce_scatter | solution.py:102
  1799.9 40.2 %all-reduce = (f32[]{:T(128)}, f32[]{:T(128)}) all-reduce(f32[]{:T(128)} %get-tuple-element.369, f32[]{:T(128)S(6)} %add.85), channel_id=1, replica_groups=mesh['stage'=4,'data'=8] {'stage','data'}, use_global_device_ids=true, to_apply=%region_7.8 | all-reduce | flops 2 | bytes 16 | tf_op jit(solution)/shard_map/psum | solution.py:107
  (173 shorter events, 425.2 us)
Async XLA Ops:
  7.2 1477.7 %reduce-scatter.5.cloned.1.call-start = ((), (), s32[]{:S(2)}) async-start(), calls=%async_computation.3 | async-start | bytes 61931520 | tf_op jit(solution)/shard_map/reduce_scatter | solution.py:103
  67.8 9.2 collective-permute-start.1
  69.1 9.1 collective-permute-start
  102.1 8.8 collective-permute-start.1
  103.4 8.7 collective-permute-start
  136.1 8.7 collective-permute-start.1
  137.4 8.2 collective-permute-start
  169.5 8.7 collective-permute-start.1
  170.8 8.2 collective-permute-start
  182.5 29.1 %collective-permute-start.1 = (bf16[64,1536]{1,0:T(8,128)(2,1)}, bf16[64,1536]{1,0:T(8,128)(2,1)S(1)}, u32[]{:S(2)}, u32[]{:S(2)}) collective-permute-start(bf16[64,1536]{1,0:T(8,128)(2,1)} %get-tuple-element.502), channel_id=1, source_target_pairs={{8,0},{16,8},{24,16},{9,1},{17,9},{25,17},{10,2},{18,10},{26,18},{... | collective-permute-start | bytes 589832 | tf_op jit(solution)/shard_map/while/body/eval_jaxpr/ppermute | solution.py:89
  183.8 28.6 %collective-permute-start = (bf16[64,1536]{1,0:T(8,128)(2,1)}, bf16[64,1536]{1,0:T(8,128)(2,1)S(1)}, u32[]{:S(2)}, u32[]{:S(2)}) collective-permute-start(bf16[64,1536]{1,0:T(8,128)(2,1)} %copy-done.1), channel_id=1, source_target_pairs={{0,8},{8,16},{16,24},{1,9},{9,17},{17,25},{2,10},{10,18},{18,26},{... | collective-permute-start | bytes 589832 | tf_op jit(solution)/shard_map/while/body/eval_jaxpr/ppermute | solution.py:88
  215.9 354.0 %collective-permute-start.1 = (bf16[64,1536]{1,0:T(8,128)(2,1)}, bf16[64,1536]{1,0:T(8,128)(2,1)S(1)}, u32[]{:S(2)}, u32[]{:S(2)}) collective-permute-start(bf16[64,1536]{1,0:T(8,128)(2,1)} %get-tuple-element.502), channel_id=1, source_target_pairs={{8,0},{16,8},{24,16},{9,1},{17,9},{25,17},{10,2},{18,10},{26,18},{... | collective-permute-start | bytes 589832 | tf_op jit(solution)/shard_map/while/body/eval_jaxpr/ppermute | solution.py:89
  217.2 353.5 %collective-permute-start = (bf16[64,1536]{1,0:T(8,128)(2,1)}, bf16[64,1536]{1,0:T(8,128)(2,1)S(1)}, u32[]{:S(2)}, u32[]{:S(2)}) collective-permute-start(bf16[64,1536]{1,0:T(8,128)(2,1)} %copy-done.1), channel_id=1, source_target_pairs={{0,8},{8,16},{16,24},{1,9},{9,17},{17,25},{2,10},{10,18},{18,26},{... | collective-permute-start | bytes 589832 | tf_op jit(solution)/shard_map/while/body/eval_jaxpr/ppermute | solution.py:88
  690.0 29.1 %collective-permute-start.1 = (bf16[64,1536]{1,0:T(8,128)(2,1)}, bf16[64,1536]{1,0:T(8,128)(2,1)S(1)}, u32[]{:S(2)}, u32[]{:S(2)}) collective-permute-start(bf16[64,1536]{1,0:T(8,128)(2,1)} %get-tuple-element.502), channel_id=1, source_target_pairs={{8,0},{16,8},{24,16},{9,1},{17,9},{25,17},{10,2},{18,10},{26,18},{... | collective-permute-start | bytes 589832 | tf_op jit(solution)/shard_map/while/body/eval_jaxpr/ppermute | solution.py:89
  691.2 28.6 %collective-permute-start = (bf16[64,1536]{1,0:T(8,128)(2,1)}, bf16[64,1536]{1,0:T(8,128)(2,1)S(1)}, u32[]{:S(2)}, u32[]{:S(2)}) collective-permute-start(bf16[64,1536]{1,0:T(8,128)(2,1)} %copy-done.1), channel_id=1, source_target_pairs={{0,8},{8,16},{16,24},{1,9},{9,17},{17,25},{2,10},{10,18},{18,26},{... | collective-permute-start | bytes 589832 | tf_op jit(solution)/shard_map/while/body/eval_jaxpr/ppermute | solution.py:88
  839.1 8.7 collective-permute-start.1
  840.4 8.2 collective-permute-start
  967.8 28.0 %collective-permute-start.1 = (bf16[64,1536]{1,0:T(8,128)(2,1)}, bf16[64,1536]{1,0:T(8,128)(2,1)S(1)}, u32[]{:S(2)}, u32[]{:S(2)}) collective-permute-start(bf16[64,1536]{1,0:T(8,128)(2,1)} %get-tuple-element.502), channel_id=1, source_target_pairs={{8,0},{16,8},{24,16},{9,1},{17,9},{25,17},{10,2},{18,10},{26,18},{... | collective-permute-start | bytes 589832 | tf_op jit(solution)/shard_map/while/body/eval_jaxpr/ppermute | solution.py:89
  969.1 27.5 %collective-permute-start = (bf16[64,1536]{1,0:T(8,128)(2,1)}, bf16[64,1536]{1,0:T(8,128)(2,1)S(1)}, u32[]{:S(2)}, u32[]{:S(2)}) collective-permute-start(bf16[64,1536]{1,0:T(8,128)(2,1)} %copy-done.1), channel_id=1, source_target_pairs={{0,8},{8,16},{16,24},{1,9},{9,17},{17,25},{2,10},{10,18},{18,26},{... | collective-permute-start | bytes 589832 | tf_op jit(solution)/shard_map/while/body/eval_jaxpr/ppermute | solution.py:88
  1115.9 8.2 collective-permute-start.1
  1117.2 7.7 collective-permute-start
  1179.4 613.8 %reduce-scatter.3.cloned.1.call-start = ((), (), s32[]{:S(2)}) async-start(), calls=%async_computation.2 | async-start | bytes 61931520 | tf_op jit(solution)/shard_map/reduce_scatter | solution.py:102
  1793.2 54.7 %slice-start = ((s8[6881280]{0:T(1024)(128)(4,1)}), s8[2686976]{0:T(1024)(128)(4,1)S(1)}, s32[]{:S(2)}) async-start(s8[6881280]{0:T(1024)(128)(4,1)} %bitcast.58), calls=%async_computation.4 | async-start | bytes 5373952
  1841.4 6.5 slice-start.1
  (14 other events, 20.4 us)
Sparse Core Ops, SparseCore 0:
  1179.5 305.3 reduce-scatter.4
  1488.5 304.6 reduce-scatter.2
where the time goes:
time: 1860 us
  waiting for transfers between devices  618 us (33%)
  matrix products  545 us (29%)
  starting transfers between devices  468 us (25%)
  local copies, waits for them, and re-layouts  106 us (6%)
  other arithmetic  57.6 us (3%)
  blocking collectives  40.2 us (2%)
    ppermute x10, starting transfers between devices, tick_body(): recv_fwd = lax.ppermute(h_end, 'stage', fwd_perm)  455 us
    reduce_scatter x1, waiting for transfers between devices, device_step(): lax.psum_scatter(jnp.stack(final_state[4]), 'data', scatter_dimension=2,...  304 us
    reduce_scatter x1, waiting for transfers between devices, device_step(): lax.psum_scatter(jnp.stack(final_state[3]), 'data', scatter_dimension=1,...  303 us
    dot_general x4, matrix products, layer_bwd(): jnp.einsum('td,tf->df', hidden, grad_pre, preferred_element_type=jnp.floa...  153 us
    dot_general x4, matrix products, layer_bwd(): jnp.einsum('tf,td->fd', gelu_out, g_out, preferred_element_type=jnp.float32)  153 us
    dot_general x4, matrix products, layer_fwd(): jnp.einsum('tf,fd->td', gelu_out, w_down_l, preferred_element_type=jnp.fl...  81.8 us
    dot_general x4, matrix products, layer_bwd(): jnp.einsum('tf,df->td', grad_pre, w_up_l, preferred_element_type=jnp.floa...  56.6 us
    while x1, local copies, waits for them, and re-layouts, device_step(): final_state = lax.fori_loop(0, n_ticks, tick_body, init_state)  54.5 us
  transfers between devices with their start and end apart: 22, of which 14 were waited for; matrix products, arithmetic and copies ran while one was open for 1% of the time, Pallas kernels for 0%

commit v1 on v0

v1 whole, which is shorter than its diff:
```python
import functools

import jax
import jax.numpy as jnp
from jax import lax
from jax.experimental import pallas as pl
from jax.experimental.pallas import tpu as pltpu
from jax.sharding import PartitionSpec as P

F32 = jnp.float32
BF16 = jnp.bfloat16
MESH = pl.DeviceIdType.MESH
K0 = 0.7978845608028654
K1 = 0.044715


def mm(a, b, dims):
    return lax.dot_general(a, b, (dims, ((), ())), preferred_element_type=F32)


def gelu_grad(u):
    uu = u * u
    t = jnp.tanh(K0 * u * (1.0 + K1 * uu))
    return 0.5 * (1.0 + t) + (0.5 * K0) * u * (1.0 - t * t) * (1.0 + 3.0 * K1 * uu)


def gelu(u):
    t = jnp.tanh(K0 * (u + K1 * (u * u * u)))
    return (u * (0.5 * (1.0 + t))).astype(BF16)


def f_tiles(half):
    first = (half + 511) // 512 * 256
    return [(0, first), (first, half - first)]


def chain_kernel(n_stages, total, x_ref, y_ref, w1_ref, w2_ref, hall, gall, loss_ref,
                 w1, w2, hbuf, gbuf, ubuf, pf, pb, rf, rb, yv, hsend, gsend,
                 s_w, s_l, s_h, r_h, s_g, r_g, s_x, r_x, s_p, r_p, s_a, r_a, s_f, r_f):
    stage = lax.axis_index("stage")
    data = lax.axis_index("data")
    chip, core = data // 2, data % 2
    nc, rows2, dim = hbuf.shape
    rows = rows2 // 2
    half = w1.shape[1]
    nchip = hall.shape[0]
    partner = (stage, chip * 2 + (1 - core))
    last = n_stages - 1
    mine = pl.ds(pl.multiple_of(core * rows, rows), rows)
    theirs = pl.ds(pl.multiple_of((1 - core) * rows, rows), rows)
    foff = pl.multiple_of(core * half, 128)
    tiles = f_tiles(half)

    def rc(src, dst, ss, rs, dev):
        return pltpu.make_async_remote_copy(
            src_ref=src, dst_ref=dst, send_sem=ss, recv_sem=rs, device_id=dev, device_id_type=MESH)

    wcopies = [
        pltpu.make_async_copy(w1_ref.at[0, :, pl.ds(foff, half)], w1, s_w.at[0]),
        pltpu.make_async_copy(w2_ref.at[0, pl.ds(foff, half), :], w2, s_w.at[1]),
    ]

    @pl.when(stage == 0)
    def _():
        for j in range(nc):
            pltpu.make_async_copy(x_ref.at[j], hbuf.at[j, mine], s_l.at[j]).start()

    for c in wcopies:
        c.start()

    @pl.when(stage == last)
    def _():
        for j in range(nc):
            pltpu.make_async_copy(y_ref.at[j], yv.at[j], s_l.at[j]).start()

    @pl.when(stage == 0)
    def _():
        for j in range(nc):
            pltpu.make_async_copy(x_ref.at[j], hbuf.at[j, mine], s_l.at[j]).wait()

    @pl.when(stage == last)
    def _():
        for j in range(nc):
            pltpu.make_async_copy(y_ref.at[j], yv.at[j], s_l.at[j]).wait()

    loss_ref[...] = jnp.zeros_like(loss_ref)

    def share(kind, buf, j):
        return rc(buf.at[j, mine], buf.at[j, mine], s_x.at[kind, j], r_x.at[kind, j], partner)

    def spread(kind, buf, allr, j, o):
        other = (chip + o) % nchip
        return rc(buf.at[j, mine], allr.at[chip, j, mine], s_a.at[kind, j, o], r_a.at[kind, j, o],
                  (stage, other * 2 + core))

    def arrived(kind, buf, allr, j, o):
        src = (chip + nchip - o) % nchip
        return rc(buf.at[j, mine], allr.at[src, j, mine], s_a.at[kind, j, o], r_a.at[kind, j, o], partner)

    def forward(kind, allr, j, o):
        src = (chip + nchip - o) % nchip
        return rc(allr.at[src, j, mine], allr.at[src, j, mine], s_f.at[kind, j, o], r_f.at[kind, j, o], partner)

    def own(kind, buf, allr, j):
        return pltpu.make_async_copy(buf.at[j], allr.at[chip, j], s_f.at[kind, j, 0])

    def hand_up(j):
        return rc(hsend.at[j], hbuf.at[j, mine], s_h.at[j], r_h.at[j], (jnp.minimum(stage + 1, last), data))

    def hand_down(j):
        return rc(gsend.at[j], gbuf.at[j, mine], s_g.at[j], r_g.at[j], (jnp.maximum(stage - 1, 0), data))

    def partial(kind, src, dst, j):
        return rc(src.at[j, theirs], dst.at[j], s_p.at[kind, j], r_p.at[kind, j], partner)

    def enter(kind, buf, allr, j):
        share(kind, buf, j).start()
        for o in range(1, nchip):
            spread(kind, buf, allr, j, o).start()
        share(kind, buf, j).wait_recv()
        own(kind, buf, allr, j).start()

    def fwd(j):
        @pl.when(stage > 0)
        def _():
            hand_up(j).wait_recv()

        enter(0, hbuf, hall, j)

        @pl.when(j == 0)
        def _():
            for c in wcopies:
                c.wait()

        h = hbuf[j]
        for i, (f0, fw) in enumerate(tiles):
            u = mm(h, w1[:, f0:f0 + fw], ((1,), (0,)))
            ubuf[j, :, f0:f0 + fw] = u
            p = mm(gelu(u), w2[f0:f0 + fw, :], ((1,), (0,)))
            if i == 0:
                pf[j] = p
            else:
                pf[j] += p
        partial(0, pf, rf, j).start()
        partial(0, pf, rf, j).wait_recv()
        out = (hbuf[j, mine, :].astype(F32) + (pf[j, mine, :] + rf[j])).astype(BF16)

        @pl.when(stage < last)
        def _():
            hsend[j] = out
            hand_up(j).start()

        @pl.when(stage == last)
        def _():
            resid = out.astype(F32) - yv[j].astype(F32)
            gbuf[j, mine, :] = (resid / total).astype(BF16)
            loss_ref[...] += jnp.sum(resid * resid).reshape(1, 1)

    def bwd(j):
        @pl.when(stage < last)
        def _():
            hand_down(j).wait_recv()

        enter(1, gbuf, gall, j)

        @pl.when(stage > 0)
        def _():
            g = gbuf[j]
            for i, (f0, fw) in enumerate(tiles):
                e = mm(g, w2[f0:f0 + fw, :], ((1,), (1,)))
                q = (e * gelu_grad(ubuf[j, :, f0:f0 + fw])).astype(BF16)
                p = mm(q, w1[:, f0:f0 + fw], ((1,), (1,)))
                if i == 0:
                    pb[j] = p
                else:
                    pb[j] += p
            partial(1, pb, rb, j).start()
            partial(1, pb, rb, j).wait_recv()
            gsend[j] = (gbuf[j, mine, :].astype(F32) + (pb[j, mine, :] + rb[j])).astype(BF16)
            hand_down(j).start()

    is_last = jnp.where(stage == last, 1, 0)

    def step(t, carry):
        j = is_last * (t // 2) + (1 - is_last) * (t % nc)
        back = is_last * (t % 2) + (1 - is_last) * (t // nc)

        @pl.when(back == 0)
        def _():
            fwd(j)

        @pl.when(back == 1)
        def _():
            bwd(j)

        return carry

    lax.fori_loop(0, 2 * nc, step, 0)

    kinds = ((0, hbuf, hall), (1, gbuf, gall))
    for kind, buf, allr in kinds:
        for j in range(nc):
            for o in range(1, nchip):
                arrived(kind, buf, allr, j, o).wait_recv()
                forward(kind, allr, j, o).start()
    for kind, buf, allr in kinds:
        for j in range(nc):
            own(kind, buf, allr, j).wait()
            share(kind, buf, j).wait_send()
            for o in range(1, nchip):
                spread(kind, buf, allr, j, o).wait_send()
                forward(kind, allr, j, o).wait_send()
                rc(allr.at[(chip + nchip - o) % nchip, j, theirs], allr.at[(chip + nchip - o) % nchip, j, theirs],
                   s_f.at[kind, j, o], r_f.at[kind, j, o], partner).wait_recv()
    for j in range(nc):
        partial(0, pf, rf, j).wait_send()

    @pl.when(stage > 0)
    def _():
        for j in range(nc):
            partial(1, pb, rb, j).wait_send()
            hand_down(j).wait_send()

    @pl.when(stage < last)
    def _():
        for j in range(nc):
            hand_up(j).wait_send()


def run_chain(tokens_in, targets, w_up, w_down, n_stages, n_data):
    nc, rows, dim = tokens_in.shape
    half = w_up.shape[2] // 2
    nchip = n_data // 2
    total = nc * rows * n_data
    any_spec = pl.BlockSpec(memory_space=pl.ANY)
    dma = pltpu.SemaphoreType.DMA
    return pl.pallas_call(
        functools.partial(chain_kernel, n_stages, total),
        out_shape=(
            jax.ShapeDtypeStruct((nchip, nc, 2 * rows, dim), BF16),
            jax.ShapeDtypeStruct((nchip, nc, 2 * rows, dim), BF16),
            jax.ShapeDtypeStruct((8, 128), F32),
        ),
        in_specs=[any_spec] * 4,
        out_specs=(any_spec, any_spec, pl.BlockSpec(memory_space=pltpu.VMEM)),
        scratch_shapes=[
            pltpu.VMEM((dim, half), BF16),
            pltpu.VMEM((half, dim), BF16),
            pltpu.VMEM((nc, 2 * rows, dim), BF16),
            pltpu.VMEM((nc, 2 * rows, dim), BF16),
            pltpu.VMEM((nc, 2 * rows, half), F32),
            pltpu.VMEM((nc, 2 * rows, dim), F32),
            pltpu.VMEM((nc, 2 * rows, dim), F32),
            pltpu.VMEM((nc, rows, dim), F32),
            pltpu.VMEM((nc, rows, dim), F32),
            pltpu.VMEM((nc, rows, dim), BF16),
            pltpu.VMEM((nc, rows, dim), BF16),
            pltpu.VMEM((nc, rows, dim), BF16),
            dma((2,)), dma((nc,)), dma((nc,)), dma((nc,)), dma((nc,)), dma((nc,)),
            dma((2, nc)), dma((2, nc)), dma((2, nc)), dma((2, nc)),
            dma((2, nc, nchip)), dma((2, nc, nchip)), dma((2, nc, nchip)), dma((2, nc, nchip)),
        ],
        compiler_params=pltpu.CompilerParams(has_side_effects=True, vmem_limit_bytes=67043328),
        name="chain",
    )(tokens_in, targets, w_up, w_down)


TILE = 1280
TOKENS = 512


def grad_kernel(n_stages, hall, gall, w1_ref, w2_ref, loss_ref, up_o, down_o, stat_o,
                hv, gv, ht, gt, w1b, w2b, upa, upx, dna, dnx, red1, red2, red3,
                s_in, s_w, s_o, s_s, r_s, s_r, r_r):
    stage = lax.axis_index("stage")
    data = lax.axis_index("data")
    chip, core = data // 2, data % 2
    total, dim = hv.shape
    part, half = upa.shape
    nchip = red2.shape[0]
    partner = (stage, chip * 2 + (1 - core))
    foff = pl.multiple_of(core * half, 128)
    mine = pl.ds(pl.multiple_of(core * part, 16), part)
    theirs = pl.ds(pl.multiple_of((1 - core) * part, 16), part)
    n_full, tail = half // TILE, half % TILE
    n_tiles = n_full + (1 if tail else 0)

    def rc(src, dst, ss, rs, dev):
        return pltpu.make_async_remote_copy(
            src_ref=src, dst_ref=dst, send_sem=ss, recv_sem=rs, device_id=dev, device_id_type=MESH)

    def loads(i, fw):
        slot = i % 2
        src = pl.ds(pl.multiple_of(foff + i * TILE, 128), fw)
        return (
            pltpu.make_async_copy(w1_ref.at[0, :, src], w1b.at[slot, :, pl.ds(0, fw)], s_w.at[slot, 0]),
            pltpu.make_async_copy(w2_ref.at[0, src, :], w2b.at[slot, pl.ds(0, fw), :], s_w.at[slot, 1]),
        )

    def start_load(i, fw):
        for c in loads(i, fw):
            c.start()

    load_h = pltpu.make_async_copy(hall, hv, s_in.at[0])
    load_g = pltpu.make_async_copy(gall, gv, s_in.at[1])
    load_h.start()
    load_g.start()
    start_load(0, TILE)
    stat_o[0] = jnp.zeros((8, 128), F32)
    stat_o[1] = loss_ref[...]
    cols = pl.ds(pl.multiple_of(chip * (2 * part), 128), 2 * part)
    load_h.wait()
    load_g.wait()
    for c in range(total // TOKENS):
        r = slice(c * TOKENS, (c + 1) * TOKENS)
        ht[:, r] = hv[r, cols].T
        gt[:, r] = gv[r, cols].T

    def outs(i, fw):
        fs = pl.ds(pl.multiple_of(i * TILE, 128), fw)
        dst = pl.ds(pl.multiple_of(foff + i * TILE, 128), fw)
        return (
            pltpu.make_async_copy(upa.at[:, fs], up_o.at[:, dst], s_o.at[i, 0]),
            pltpu.make_async_copy(dna.at[:, fs], down_o.at[:, dst], s_o.at[i, 1]),
            rc(upx.at[:, fs], up_o.at[:, dst], s_s.at[i, 0], r_s.at[i, 0], partner),
            rc(dnx.at[:, fs], down_o.at[:, dst], s_s.at[i, 1], r_s.at[i, 1], partner),
        )

    def compute(i, fw):
        slot = i % 2
        fs = pl.ds(pl.multiple_of(i * TILE, 128), fw)
        for c in loads(i, fw):
            c.wait()
        for buf in (upa, upx, dna, dnx):
            buf[:, fs] = jnp.zeros((part, fw), F32)

        def chunk(c, carry):
            r = pl.ds(pl.multiple_of(c * TOKENS, TOKENS), TOKENS)
            u = mm(hv[r, :], w1b[slot, :, :fw], ((1,), (0,)))
            e = mm(gv[r, :], w2b[slot, :fw, :], ((1,), (1,)))
            uu = u * u
            t = jnp.tanh(K0 * u * (1.0 + K1 * uu))
            cdf = 0.5 * (1.0 + t)
            a = (u * cdf).astype(BF16)
            q = (e * (cdf + (0.5 * K0) * u * (1.0 - t * t) * (1.0 + 3.0 * K1 * uu))).astype(BF16)
            dna[:, fs] += mm(gt[mine, r], a, ((1,), (0,)))
            dnx[:, fs] += mm(gt[theirs, r], a, ((1,), (0,)))
            upa[:, fs] += mm(ht[mine, r], q, ((1,), (0,)))
            upx[:, fs] += mm(ht[theirs, r], q, ((1,), (0,)))
            return carry

        lax.fori_loop(0, total // TOKENS, chunk, 0)
        for c in outs(i, fw):
            c.start()
        acc = jnp.zeros((8, fw), F32)
        for buf in (upa, upx, dna, dnx):
            v = buf[:, fs]
            acc += jnp.sum((v * v).reshape(part // 8, 8, fw), axis=0)
        sq = acc[:, :128]
        for k in range(1, fw // 128):
            sq += acc[:, k * 128:(k + 1) * 128]
        stat_o[0] += sq

    def tile_step(i, carry):
        @pl.when(i + 1 < n_full)
        def _():
            start_load(i + 1, TILE)

        if tail:
            @pl.when(i + 1 == n_full)
            def _():
                start_load(i + 1, tail)

        compute(i, TILE)
        return carry

    lax.fori_loop(0, n_full, tile_step, 0)
    if tail:
        compute(n_full, tail)

    red1[core] = stat_o[...]
    c1 = rc(red1.at[core], red1.at[core], s_r.at[0, 0], r_r.at[0, 0], partner)
    c1.start()
    c1.wait()
    red2[chip] = red1[0] + red1[1]

    def to_chip(o):
        return rc(red2.at[chip], red2.at[chip], s_r.at[1, o], r_r.at[1, o],
                  (stage, ((chip + o) % nchip) * 2 + core))

    def to_stage(o):
        return rc(red3.at[stage], red3.at[stage], s_r.at[2, o], r_r.at[2, o], ((stage + o) % n_stages, data))

    for o in range(1, nchip):
        to_chip(o).start()
    for o in range(1, nchip):
        to_chip(o).wait()
    v = red2[0]
    for k in range(1, nchip):
        v = v + red2[k]
    red3[stage] = v
    for o in range(1, n_stages):
        to_stage(o).start()
    for o in range(1, n_stages):
        to_stage(o).wait()
    v = red3[0]
    for k in range(1, n_stages):
        v = v + red3[k]
    stat_o[...] = v
    for i in range(n_tiles):
        for c in outs(i, TILE if i < n_full else tail):
            c.wait()


def run_grads(h_all, g_all, w_up, w_down, loss, n_stages, n_data):
    total, dim = h_all.shape
    ffn = w_up.shape[2]
    half = ffn // 2
    part = dim // n_data
    nchip = n_data // 2
    n_tiles = -(-half // TILE)
    any_spec = pl.BlockSpec(memory_space=pl.ANY)
    vmem = pl.BlockSpec(memory_space=pltpu.VMEM)
    dma = pltpu.SemaphoreType.DMA
    peers = max(nchip, n_stages)
    return pl.pallas_call(
        functools.partial(grad_kernel, n_stages),
        out_shape=(
            jax.ShapeDtypeStruct((part, ffn), F32),
            jax.ShapeDtypeStruct((part, ffn), F32),
            jax.ShapeDtypeStruct((2, 8, 128), F32),
        ),
        in_specs=[any_spec] * 4 + [vmem],
        out_specs=(any_spec, any_spec, vmem),
        scratch_shapes=[
            pltpu.VMEM((total, dim), BF16),
            pltpu.VMEM((total, dim), BF16),
            pltpu.VMEM((2 * part, total), BF16),
            pltpu.VMEM((2 * part, total), BF16),
            pltpu.VMEM((2, dim, TILE), BF16),
            pltpu.VMEM((2, TILE, dim), BF16),
            pltpu.VMEM((part, half), F32),
            pltpu.VMEM((part, half), F32),
            pltpu.VMEM((part, half), F32),
            pltpu.VMEM((part, half), F32),
            pltpu.VMEM((2, 2, 8, 128), F32),
            pltpu.VMEM((nchip, 2, 8, 128), F32),
            pltpu.VMEM((n_stages, 2, 8, 128), F32),
            dma((2,)), dma((2, 2)), dma((n_tiles, 2)), dma((n_tiles, 2)), dma((n_tiles, 2)),
            dma((3, peers)), dma((3, peers)),
        ],
        compiler_params=pltpu.CompilerParams(has_side_effects=True, vmem_limit_bytes=67043328),
        name="grads",
    )(h_all, g_all, w_up, w_down, loss)


def solution(mesh):
    n_stages = mesh.shape["stage"]
    n_data = mesh.shape["data"]

    def device_step(tokens_in, targets, w_up, w_down, clip_norm):
        n_micro, n_tokens, dim = tokens_in.shape
        total = n_micro * n_tokens * n_data
        h_all, g_all, loss = run_chain(tokens_in, targets, w_up, w_down, n_stages, n_data)
        up, down, stat = run_grads(h_all.reshape(total, dim), g_all.reshape(total, dim), w_up, w_down, loss,
                                   n_stages, n_data)
        scale = jnp.minimum(1.0, clip_norm / jnp.sqrt(jnp.sum(stat[0])))
        return stat[1, 0, 0] / (2 * total), (up * scale)[None], (down * scale).T[None]

    return jax.shard_map(
        device_step,
        mesh=mesh,
        in_specs=(P("data"), P("data"), P("stage"), P("stage"), P()),
        out_specs=(P(), P("stage", "data", None), P("stage", None, "data")),
        check_vma=False,
    )
```

time: 1860 us -> 299 us (0.16)
  waiting for transfers between devices: 618 us -> 0 us
  matrix products: 545 us -> 0 us
  starting transfers between devices: 468 us -> 0 us
  Pallas kernels: 0 us -> 282 us
  local copies, waits for them, and re-layouts: 106 us -> 1.19 us
  other arithmetic: 57.6 us -> 12.2 us
  blocking collectives: 40.2 us -> 0 us
    reduce_scatter x2 -> x0, waiting for transfers between devices: 607 us -> none  [the longest x1 304 us: device_step(): lax.psum_scatter(jnp.stack(final_state[4]), 'data', scatter_dimension=2,...]
    dot_general x24 -> x0, matrix products: 545 us -> none  [the longest x4 153 us: layer_bwd(): jnp.einsum('td,tf->df', hidden, grad_pre, preferred_element_type=jnp.floa...]
    ppermute x20 -> x0, starting transfers between devices: 468 us -> none  [the longest x10 455 us: tick_body(): recv_fwd = lax.ppermute(h_end, 'stage', fwd_perm)]
    pallas_call x0 -> x2, Pallas kernels: none -> 282 us  [the longest x1 179 us: run_chain(): pl.pallas_call(functools.partial(chain_kernel, n_stages, total), out_shap...]
    while x21 -> x0, local copies, waits for them, and re-layouts: 54.5 us -> none  [the longest x1 54.5 us: device_step(): final_state = lax.fori_loop(0, n_ticks, tick_body, init_state)]
    psum x1 -> x0, blocking collectives: 40.2 us -> none  [device_step(): lax.psum(final_state[5], ('stage', 'data')) / (2 * total_tokens)]
    broadcast_in_dim x11 -> x0, local copies, waits for them, and re-layouts: 36.7 us -> none  [the longest x1 17.8 us: device_step(): jnp.zeros((ffn_dim, model_dim), jnp.float32)]
    reduce_sum x12 -> x1, other arithmetic: 28.2 us -> 1.28 us  [device_step(): scale = jnp.minimum(1.0, clip_norm / jnp.sqrt(jnp.sum(stat[0])))]
  transfers between devices with their start and end apart: 22 -> 0, of which waited for: 14 -> 0; matrix products, arithmetic and copies ran while one was open for 1% -> 0% of each run, Pallas kernels for 0% -> 0%
where the time goes in v1:
time: 299 us
  Pallas kernels  282 us (94%)
  other arithmetic  12.2 us (4%)
  between operations  3.77 us (1%)
    pallas_call x1, Pallas kernels, run_chain(): pl.pallas_call(functools.partial(chain_kernel, n_stages, total), out_shap...  179 us
    pallas_call x1, Pallas kernels, run_grads(): pl.pallas_call(functools.partial(grad_kernel, n_stages), out_shape=(jax.S...  102 us
    broadcast_in_dim x1, other arithmetic, device_step(): (down * scale).T[None]  11 us

profile of v1, /device:TPU:0, one launch (start us, length us, event | category | flops | bytes accessed | tf_op | source)
XLA Modules:
  0.0 298.8 jit_solution(14176567217497085729)
XLA Ops:
  1.3 179.4 %chain.1 = (bf16[4,4,128,1536]{3,2,1,0:T(8,128)(2,1)}, bf16[4,4,128,1536]{3,2,1,0:T(8,128)(2,1)}, f32[8,128]{1,0:T(8,128)}) custom-call(bf16[4,64,1536]{2,1,0:T(8,128)(2,1)} %x_ref.1, bf16[4,64,1536]{2,1,0:T(8,128)(2,1)} %y_ref.1, bf16[1,1536,8960]{2,1,0:T(8,128)(2,1)} %w1_ref.3, bf16[1,8960,1536]{2,1,0:T(8,128)(2,1)} %w2_ref.3), custom_call_target="tpu_custom_call" | custom-call | tf_op jit(solution)/shard_map/chain/pallas_call | solution.py:237
  180.7 102.3 %grads.1 = (f32[192,8960]{1,0:T(8,128)}, f32[192,8960]{1,0:T(8,128)}, f32[2,8,128]{2,1,0:T(8,128)}) custom-call(bf16[2048,1536]{1,0:T(8,128)(2,1)} %bitcast.9, bf16[2048,1536]{1,0:T(8,128)(2,1)} %bitcast.10, bf16[1,1536,8960]{2,1,0:T(8,128)(2,1)} %w1_ref.3, bf16[1,8960,1536]{2,1,0:T(8,128)(2,1)} %w2_ref.3, f32[8,128]{1,0:T(8,128)} %get-tuple-element.11.loss_ref), custom_call_target="tpu_custom_call" | custom-call | tf_op jit(solution)/shard_map/grads/pallas_call | solution.py:426
  282.9 1.3 slice_reduce_fusion
  284.9 1.2 slice.6
  286.7 11.0 %multiply_bitcast_fusion = (f32[1,8960,192]{1,2,0:T(8,128)}, f32[1,192,8960]{2,1,0:T(8,128)}) fusion(f32[192,8960]{1,0:T(8,128)} %get-tuple-element.14, f32[]{:T(128)S(6)} %min_shard_map.3, f32[192,8960]{1,0:T(8,128)} %get-tuple-element.13), kind=kLoop, calls=%fused_computation | loop fusion | flops 3440640 | bytes 27525124 | tf_op jit(solution)/shard_map/broadcast_in_dim | solution.py:468
